TPU v7x, 32 devices: a whole 2x2x4 slice. The times are simulated.
32 devices in a mesh: job: 2 (over core), replica: 4 (over z), model: 4 (over y, x).
Axes of the slice: x: 2, y: 2, z: 4, core: 2. Of those that a mesh axis runs over, the one named last changes fastest.
Arguments:
- grad_query: float32 [8, 1024, 1024], P(('job', 'replica'), None, 'model'), parts along dimension 0, may hold values from -0.875 to 0.875
- grad_key: float32 [8, 1024, 1024], P(('job', 'replica'), None, 'model'), parts along dimension 0, may hold values from -0.875 to 0.875
- grad_value: float32 [8, 1024, 1024], P(('job', 'replica'), None, 'model'), parts along dimension 0, may hold values from -0.875 to 0.875
- grad_mixed: float32 [8, 1024, 1024], P(('job', 'replica'), 'model'), parts along dimension 0, may hold values from -0.875 to 0.875
- grad_norm: float32 [8, 1024], P(('job', 'replica')), parts along dimension 0, may hold values from -8 to 8
- weight_query: float32 [2048, 1024], P(('job', 'replica'), 'model'), parts along dimension 0, may hold values from -0.25 to 0.25
- weight_key: float32 [2048, 1024], P(('job', 'replica'), 'model'), parts along dimension 0, may hold values from -0.25 to 0.25
- weight_value: float32 [2048, 1024], P(('job', 'replica'), 'model'), parts along dimension 0, may hold values from -0.25 to 0.25
- weight_mixed: float32 [2048, 1024], P(('job', 'model'), 'replica'), parts along dimension 0, may hold values from -0.25 to 0.25
- weight_norm: float32 [2048], P(('job', 'replica')), parts along dimension 0, may hold values from 0.25 to 1.75
- moment_query: float32 [2048, 1024], P(('job', 'replica'), 'model'), parts along dimension 0, may hold values from -0.1875 to 0.1875
- moment_key: float32 [2048, 1024], P(('job', 'replica'), 'model'), parts along dimension 0, may hold values from -0.1875 to 0.1875
- moment_value: float32 [2048, 1024], P(('job', 'replica'), 'model'), parts along dimension 0, may hold values from -0.1875 to 0.1875
- moment_mixed: float32 [2048, 1024], P(('job', 'model'), 'replica'), parts along dimension 0, may hold values from -0.1875 to 0.1875
- moment_norm: float32 [2048], P(('job', 'replica')), parts along dimension 0, may hold values from -1.75 to 1.75
Outputs:
- copy_query: bfloat16 [2048, 1024], P('job', 'model'), parts along dimension 0
- copy_key: bfloat16 [2048, 1024], P('job', 'model'), parts along dimension 0
- copy_value: bfloat16 [2048, 1024], P('job', 'model'), parts along dimension 0
- copy_mixed: bfloat16 [2048, 1024], P(('job', 'model')), parts along dimension 0
- copy_norm: bfloat16 [2048], P('job'), parts along dimension 0
- new_query: float32 [2048, 1024], P(('job', 'replica'), 'model'), parts along dimension 0
- new_key: float32 [2048, 1024], P(('job', 'replica'), 'model'), parts along dimension 0
- new_value: float32 [2048, 1024], P(('job', 'replica'), 'model'), parts along dimension 0
- new_mixed: float32 [2048, 1024], P(('job', 'model'), 'replica'), parts along dimension 0
- new_norm: float32 [2048], P(('job', 'replica')), parts along dimension 0
- state_new_query: float32 [2048, 1024], P(('job', 'replica'), 'model'), parts along dimension 0
- state_new_key: float32 [2048, 1024], P(('job', 'replica'), 'model'), parts along dimension 0
- state_new_value: float32 [2048, 1024], P(('job', 'replica'), 'model'), parts along dimension 0
- state_new_mixed: float32 [2048, 1024], P(('job', 'model'), 'replica'), parts along dimension 0
- state_new_norm: float32 [2048], P(('job', 'replica')), parts along dimension 0
There are 2 independent parts, one for each index of `job`. A program takes and returns all parts, laid end to end along the dimension named above; each array names one. Nothing has to cross between parts.
All inputs are finite; a program needn't handle non-finite values.
Results may differ from a plain program's by a relative error of at most 0.0004.
Values may be sent and summed in bfloat16 or wider, within the bound.
No kernel may reach another device: no remote copies, remote signals or barrier semaphores. Data moves between devices by JAX's collectives and lax.ppermute only.
A program may use at most 64 MiB of HBM per device.

v0:
```python
import jax
import jax.numpy as jnp
from jax import lax
from jax.sharding import PartitionSpec as P

learn_rate = 0.5
hold_rate = 0.9


def local(
    grad_query,
    grad_key,
    grad_value,
    grad_mixed,
    grad_norm,
    weight_query,
    weight_key,
    weight_value,
    weight_mixed,
    weight_norm,
    moment_query,
    moment_key,
    moment_value,
    moment_mixed,
    moment_norm,
):
    mean_query, mean_key, mean_value, mean_mixed = (
        lax.psum_scatter(grad_query[0], "replica", scatter_dimension=0, tiled=True),
        lax.psum_scatter(grad_key[0], "replica", scatter_dimension=0, tiled=True),
        lax.psum_scatter(grad_value[0], "replica", scatter_dimension=0, tiled=True),
        lax.psum_scatter(grad_mixed[0], "replica", scatter_dimension=1, tiled=True),
    )
    whole_norm = lax.psum(grad_norm[0], "replica")
    place = lax.axis_index("replica")
    mean_norm = lax.dynamic_slice_in_dim(
        whole_norm, place * weight_norm.shape[0], weight_norm.shape[0]
    )
    mean_rate = lax.axis_size("replica") ** (-0.5)
    mean_query = mean_query * mean_rate
    mean_key = mean_key * mean_rate
    mean_value = mean_value * mean_rate
    mean_mixed = mean_mixed * mean_rate
    mean_norm = mean_norm * mean_rate
    (
        own_query,
        own_key,
        own_value,
        own_mixed,
        slope_query_norm,
        slope_key_norm,
        slope_value_norm,
        slope_mixed_norm,
    ) = lax.psum(
        (
            jnp.sum(weight_query * weight_query, axis=1, keepdims=True),
            jnp.sum(weight_key * weight_key, axis=1, keepdims=True),
            jnp.sum(weight_value * weight_value, axis=1, keepdims=True),
            jnp.sum(weight_mixed * weight_mixed, axis=0, keepdims=True),
            jnp.sum(mean_query * mean_query, axis=1, keepdims=True),
            jnp.sum(mean_key * mean_key, axis=1, keepdims=True),
            jnp.sum(mean_value * mean_value, axis=1, keepdims=True),
            jnp.sum(mean_mixed * mean_mixed, axis=0, keepdims=True),
        ),
        "model",
    )
    mean_query = mean_query * (jnp.sqrt(own_query) * lax.rsqrt(slope_query_norm + 1e-06))
    mean_key = mean_key * (jnp.sqrt(own_key) * lax.rsqrt(slope_key_norm + 1e-06))
    mean_value = mean_value * (jnp.sqrt(own_value) * lax.rsqrt(slope_value_norm + 1e-06))
    mean_mixed = mean_mixed * (jnp.sqrt(own_mixed) * lax.rsqrt(slope_mixed_norm + 1e-06))
    state_new_query = hold_rate * moment_query + mean_query
    new_query = weight_query - learn_rate * state_new_query
    state_new_key = hold_rate * moment_key + mean_key
    new_key = weight_key - learn_rate * state_new_key
    state_new_value = hold_rate * moment_value + mean_value
    new_value = weight_value - learn_rate * state_new_value
    state_new_mixed = hold_rate * moment_mixed + mean_mixed
    new_mixed = weight_mixed - learn_rate * state_new_mixed
    state_new_norm = hold_rate * moment_norm + mean_norm
    new_norm = weight_norm - learn_rate * state_new_norm
    copy_query, copy_key, copy_value, copy_mixed, copy_norm = (
        lax.all_gather(new_query.astype(jnp.bfloat16), "replica", axis=0, tiled=True),
        lax.all_gather(new_key.astype(jnp.bfloat16), "replica", axis=0, tiled=True),
        lax.all_gather(new_value.astype(jnp.bfloat16), "replica", axis=0, tiled=True),
        lax.all_gather(new_mixed.astype(jnp.bfloat16), "replica", axis=1, tiled=True),
        lax.all_gather(new_norm.astype(jnp.bfloat16), "replica", axis=0, tiled=True),
    )
    return (
        copy_query,
        copy_key,
        copy_value,
        copy_mixed,
        copy_norm,
        new_query,
        new_key,
        new_value,
        new_mixed,
        new_norm,
        state_new_query,
        state_new_key,
        state_new_value,
        state_new_mixed,
        state_new_norm,
    )


def solution(mesh):
    placed = (
        P(("job", "replica"), None, "model"),
        P(("job", "replica"), None, "model"),
        P(("job", "replica"), None, "model"),
        P(("job", "replica"), "model", None),
        P(("job", "replica"), None),
        P(("job", "replica"), "model"),
        P(("job", "replica"), "model"),
        P(("job", "replica"), "model"),
        P(("job", "model"), "replica"),
        P(("job", "replica")),
        P(("job", "replica"), "model"),
        P(("job", "replica"), "model"),
        P(("job", "replica"), "model"),
        P(("job", "model"), "replica"),
        P(("job", "replica")),
    )
    return jax.shard_map(
        local,
        mesh=mesh,
        in_specs=placed,
        out_specs=(
            P("job", "model"),
            P("job", "model"),
            P("job", "model"),
            P(("job", "model"), None),
            P("job"),
            P(("job", "replica"), "model"),
            P(("job", "replica"), "model"),
            P(("job", "replica"), "model"),
            P(("job", "model"), "replica"),
            P(("job", "replica")),
            P(("job", "replica"), "model"),
            P(("job", "replica"), "model"),
            P(("job", "replica"), "model"),
            P(("job", "model"), "replica"),
            P(("job", "replica")),
        ),
        check_vma=False,
    )
```

profile of v0, /device:TPU:0, one launch (start us, length us, event | category | flops | bytes accessed | tf_op | source)
XLA Modules:
  0.0 210.1 jit_solution(8399502176376450542)
XLA Ops:
  7.2 0.0 reduce-scatter.9.cloned.1.call-start
  7.2 0.7 reduce-scatter.9.cloned.1.call-update
  7.9 0.0 reduce-scatter.11.cloned.1.call-start
  8.0 0.7 reduce-scatter.11.cloned.1.call-update
  8.7 0.0 reduce-scatter.5.cloned.1.call-start
  8.7 0.7 reduce-scatter.5.cloned.1.call-update
  9.4 0.0 reduce-scatter.7.cloned.1.call-start
  9.4 0.0 copy-start.12
  9.5 0.0 copy-start.13
  9.5 0.0 copy-start.14
  9.5 0.0 copy-start.3
  9.5 0.5 reduce-scatter.7.cloned.1.call-update
  10.0 0.0 copy-start.2
  10.0 0.1 copy-done.12
  10.1 13.5 %psum.71 = f32[1024]{0:T(1024)S(1)} all-reduce(f32[1024]{0:T(1024)S(1)} %bitcast.36), channel_id=1, replica_groups=mesh['job'=2,'replica'=4,'model'=4] {'replica'}, use_global_device_ids=true, to_apply=%region_20.0 | all-reduce | flops 1024 | bytes 8192 | tf_op jit(solution)/shard_map/psum | solution.py:33
  23.6 0.0 copy-done.13
  23.6 0.0 copy-done.14
  23.6 0.6 fusion
  24.3 7.7 %all-gather = bf16[4,1,256]{2,1,0:T(2,128)(2,1)S(1)} all-gather(bf16[1,1,256]{2,1,0:T(2,128)(2,1)S(1)} %reshape.38), channel_id=1, replica_groups=mesh['job'=2,'replica'=4,'model'=4] {'replica'}, dimensions={0}, use_global_device_ids=true | all-gather | bytes 2560 | tf_op jit(solution)/shard_map/all_gather | solution.py:85
  32.0 0.6 copy.30
  32.6 0.0 copy-done.3
  32.6 0.0 copy-start
  32.6 0.1 multiply_reduce_fusion.7
  32.7 0.0 copy-done.2
  32.7 0.0 copy-start.1
  32.7 0.1 multiply_reduce_fusion.1
  32.8 0.8 copy-done
  33.5 0.1 multiply_reduce_fusion.5
  33.7 0.0 copy-done.1
  33.7 0.1 multiply_reduce_fusion.3
  33.8 6.6 %reduce-scatter.9.cloned.1.call-done = f32[256,256]{1,0:T(8,128)} async-done(((f32[1024,256]{1,0:T(8,128)}), f32[256,256]{1,0:T(8,128)}) %reduce-scatter.9.cloned.1.call-update) | async-done | bytes 262160 | tf_op jit(solution)/shard_map/reduce_scatter | solution.py:30
  40.4 1.1 multiply_reduce_fusion.2
  41.5 27.1 %reduce-scatter.11.cloned.1.call-done = f32[256,256]{1,0:T(8,128)} async-done(((f32[256,1024]{1,0:T(8,128)}), f32[256,256]{1,0:T(8,128)}) %reduce-scatter.11.cloned.1.call-update) | async-done | bytes 262160 | tf_op jit(solution)/shard_map/reduce_scatter | solution.py:31
  68.6 1.0 multiply_reduce_fusion
  69.6 27.1 %reduce-scatter.5.cloned.1.call-done = f32[256,256]{1,0:T(8,128)} async-done(((f32[1024,256]{1,0:T(8,128)}), f32[256,256]{1,0:T(8,128)}) %reduce-scatter.5.cloned.1.call-update) | async-done | bytes 262160 | tf_op jit(solution)/shard_map/reduce_scatter | solution.py:28
  96.7 1.1 multiply_reduce_fusion.6
  97.7 26.9 %reduce-scatter.7.cloned.1.call-done = f32[256,256]{1,0:T(8,128)} async-done(((f32[1024,256]{1,0:T(8,128)}), f32[256,256]{1,0:T(8,128)}) %reduce-scatter.7.cloned.1.call-update) | async-done | bytes 262160 | tf_op jit(solution)/shard_map/reduce_scatter | solution.py:29
  124.7 0.0 copy-start.7
  124.7 1.1 multiply_reduce_fusion.4
  125.8 10.0 %all-reduce = (f32[256,1]{0,1:T(1,128)S(1)}, f32[256,1]{0,1:T(1,128)S(1)}, f32[256,1]{0,1:T(1,128)S(1)}, f32[256,1]{0,1:T(1,128)S(1)}, f32[256,1]{0,1:T(1,128)S(...) all-reduce(f32[256,1]{0,1:T(1,128)S(1)} %bitcast.34, ...), channel_id=1, replica_groups=mesh['job'=2,'replica'=4,'model'=4] {'model'}, use_global_device_ids=true, to_apply=%region_4.0 | all-reduce | flops 2048 | bytes 16384 | tf_op jit(solution)/shard_map/psum | solution.py:53
  135.8 0.0 copy-done.8
  135.8 0.0 copy-done.7
  135.8 0.9 fusion.3
  136.7 0.0 copy-start.6
  136.7 0.0 copy-start.9
  136.7 14.8 %all_gather.16 = bf16[1024,256]{1,0:T(8,128)(2,1)S(1)} all-gather(bf16[256,256]{1,0:T(8,128)(2,1)S(1)} %get-tuple-element.32), channel_id=1, replica_groups=mesh['job'=2,'replica'=4,'model'=4] {'replica'}, dimensions={0}, use_global_device_ids=true | all-gather | bytes 655360 | tf_op jit(solution)/shard_map/all_gather | solution.py:82
  151.5 0.0 copy-done.6
  151.5 0.0 copy-done.9
  151.5 0.9 fusion.2
  152.4 0.0 copy-start.5
  152.4 0.0 copy-start.10
  152.4 15.3 %all_gather.17 = bf16[1024,256]{1,0:T(8,128)(2,1)S(1)} all-gather(bf16[256,256]{1,0:T(8,128)(2,1)S(1)} %get-tuple-element.29), channel_id=1, replica_groups=mesh['job'=2,'replica'=4,'model'=4] {'replica'}, dimensions={0}, use_global_device_ids=true | all-gather | bytes 655360 | tf_op jit(solution)/shard_map/all_gather | solution.py:83
  167.8 0.0 copy-done.5
  167.8 0.0 copy-done.10
  167.8 0.8 fusion.1
  168.6 16.1 %all_gather.18 = bf16[256,1024]{1,0:T(8,128)(2,1)S(1)} all-gather(bf16[256,256]{1,0:T(8,128)(2,1)S(1)} %get-tuple-element.26), channel_id=1, replica_groups=mesh['job'=2,'replica'=4,'model'=4] {'replica'}, dimensions={1}, use_global_device_ids=true | all-gather | bytes 655360 | tf_op jit(solution)/shard_map/all_gather | solution.py:84
  184.7 0.0 copy-done.4
  184.7 0.0 copy-done.11
  184.7 0.9 fusion.4
  185.7 14.8 %all_gather.15 = bf16[1024,256]{1,0:T(8,128)(2,1)S(1)} all-gather(bf16[256,256]{1,0:T(8,128)(2,1)S(1)} %get-tuple-element.35), channel_id=1, replica_groups=mesh['job'=2,'replica'=4,'model'=4] {'replica'}, dimensions={0}, use_global_device_ids=true | all-gather | bytes 655360 | tf_op jit(solution)/shard_map/all_gather | solution.py:81
  200.4 0.8 copy.35
  201.2 0.8 copy.36
  202.0 0.8 copy.37
  202.8 0.8 copy.38
  (8 shorter events, 0.1 us)
Async XLA Ops:
  7.2 33.2 %reduce-scatter.9.cloned.1.call-start = ((), (), s32[]{:S(2)}) async-start(), calls=%async_computation.6 | async-start | bytes 1310720 | tf_op jit(solution)/shard_map/reduce_scatter | solution.py:30
  7.9 60.6 %reduce-scatter.11.cloned.1.call-start = ((), (), s32[]{:S(2)}) async-start(), calls=%async_computation.7 | async-start | bytes 1310720 | tf_op jit(solution)/shard_map/reduce_scatter | solution.py:31
  8.7 88.0 %reduce-scatter.5.cloned.1.call-start = ((), (), s32[]{:S(2)}) async-start(), calls=%async_computation.4 | async-start | bytes 1310720 | tf_op jit(solution)/shard_map/reduce_scatter | solution.py:28
  9.4 115.2 %reduce-scatter.7.cloned.1.call-start = ((), (), s32[]{:S(2)}) async-start(), calls=%async_computation.5 | async-start | bytes 1310720 | tf_op jit(solution)/shard_map/reduce_scatter | solution.py:29
  9.4 0.7 copy-start.12
  9.5 14.1 %copy-start.13 = (f32[256]{0:T(256)S(1)}, f32[256]{0:T(256)}, u32[]{:S(2)}) copy-start(f32[256]{0:T(256)} %param.24) | copy-start | bytes 3076
  9.5 14.1 %copy-start.14 = (f32[256]{0:T(256)S(1)}, f32[256]{0:T(256)}, u32[]{:S(2)}) copy-start(f32[256]{0:T(256)} %param.29) | copy-start | bytes 3076
  9.5 23.1 %copy-start.3 = (f32[256,256]{1,0:T(8,128)S(1)}, f32[256,256]{1,0:T(8,128)}, u32[]{:S(2)}) copy-start(f32[256,256]{1,0:T(8,128)} %param.20) | copy-start | bytes 786436
  10.0 22.7 %copy-start.2 = (f32[256,256]{1,0:T(8,128)S(1)}, f32[256,256]{1,0:T(8,128)}, u32[]{:S(2)}) copy-start(f32[256,256]{1,0:T(8,128)} %param.23) | copy-start | bytes 786436
  32.6 1.0 copy-start
  32.7 1.0 copy-start.1
  69.6 66.2 %copy-start.8 = (f32[256,256]{1,0:T(8,128)S(1)}, f32[256,256]{1,0:T(8,128)}, u32[]{:S(2)}) copy-start(f32[256,256]{1,0:T(8,128)} %param.26) | copy-start | bytes 786436
  124.7 11.2 %copy-start.7 = (f32[256,256]{1,0:T(8,128)S(1)}, f32[256,256]{1,0:T(8,128)}, u32[]{:S(2)}) copy-start(f32[256,256]{1,0:T(8,128)} %reduce-scatter.7.cloned.1.call-done) | copy-start | bytes 786436
  136.7 14.8 %copy-start.6 = (f32[256,256]{1,0:T(8,128)S(1)}, f32[256,256]{1,0:T(8,128)}, u32[]{:S(2)}) copy-start(f32[256,256]{1,0:T(8,128)} %reduce-scatter.9.cloned.1.call-done) | copy-start | bytes 786436
  136.7 14.8 %copy-start.9 = (f32[256,256]{1,0:T(8,128)S(1)}, f32[256,256]{1,0:T(8,128)}, u32[]{:S(2)}) copy-start(f32[256,256]{1,0:T(8,128)} %param.27) | copy-start | bytes 786436
  152.4 15.3 %copy-start.5 = (f32[256,256]{1,0:T(8,128)S(1)}, f32[256,256]{1,0:T(8,128)}, u32[]{:S(2)}) copy-start(f32[256,256]{1,0:T(8,128)} %reduce-scatter.11.cloned.1.call-done) | copy-start | bytes 786436
  152.4 15.4 %copy-start.10 = (f32[256,256]{1,0:T(8,128)S(1)}, f32[256,256]{1,0:T(8,128)}, u32[]{:S(2)}) copy-start(f32[256,256]{1,0:T(8,128)} %param.28) | copy-start | bytes 786436
  168.6 16.1 %copy-start.4 = (f32[256,256]{1,0:T(8,128)S(1)}, f32[256,256]{1,0:T(8,128)}, u32[]{:S(2)}) copy-start(f32[256,256]{1,0:T(8,128)} %reduce-scatter.5.cloned.1.call-done) | copy-start | bytes 786436
  168.6 16.1 %copy-start.11 = (f32[256,256]{1,0:T(8,128)S(1)}, f32[256,256]{1,0:T(8,128)}, u32[]{:S(2)}) copy-start(f32[256,256]{1,0:T(8,128)} %param.25) | copy-start | bytes 786436
Sparse Core Ops, SparseCore 0:
  10.3 30.1 reduce-scatter.8
  42.7 25.7 reduce-scatter.10
  70.9 25.7 reduce-scatter.4
  98.8 25.7 reduce-scatter.6
where the time goes:
time: 210 us
  blocking collectives  92.1 us (44%)
  waiting for transfers between devices  90.2 us (43%)
  between operations  14 us (7%)
  other arithmetic  8.91 us (4%)
  local copies, waits for them, and re-layouts  4.75 us (2%)
    reduce_scatter x1, waiting for transfers between devices, local(): lax.psum_scatter(grad_query[0], 'replica', scatter_dimension=0, tiled=True)  27.1 us
    reduce_scatter x1, waiting for transfers between devices, local(): lax.psum_scatter(grad_mixed[0], 'replica', scatter_dimension=1, tiled=True)  27.1 us
    reduce_scatter x1, waiting for transfers between devices, local(): lax.psum_scatter(grad_key[0], 'replica', scatter_dimension=0, tiled=True)  26.9 us
    all_gather x1, blocking collectives, local(): lax.all_gather(new_mixed.astype(jnp.bfloat16), 'replica', axis=1, tiled=T...  16.1 us
    all_gather x1, blocking collectives, local(): lax.all_gather(new_value.astype(jnp.bfloat16), 'replica', axis=0, tiled=T...  15.3 us
    all_gather x1, blocking collectives, local(): lax.all_gather(new_key.astype(jnp.bfloat16), 'replica', axis=0, tiled=True)  14.8 us
    all_gather x1, blocking collectives, local(): lax.all_gather(new_query.astype(jnp.bfloat16), 'replica', axis=0, tiled=T...  14.8 us
    psum x1, blocking collectives, local(): whole_norm = lax.psum(grad_norm[0], 'replica')  13.5 us
  transfers between devices with their start and end apart: 4, of which 4 were waited for; matrix products, arithmetic and copies ran while one was open for 2% of the time, Pallas kernels for 0%

commit v1 on v0

--- a/solution.py
+++ b/solution.py
@@ -5,6 +5,27 @@
 
 learn_rate = 0.5
 hold_rate = 0.9
+
+
+def joined_along(blocks, dim):
+    shape = list(blocks.shape[1:])
+    shape[dim] *= blocks.shape[0]
+    return jnp.moveaxis(blocks, 0, dim).reshape(shape)
+
+
+def doubled(x, axis):
+    count, index = (lax.axis_size(axis), lax.axis_index(axis))
+    pieces, stride = (x[None], 1)
+    while stride < count:
+        other = lax.ppermute(pieces, axis, [(i, i ^ stride) for i in range(count)])
+        low = index & stride == 0
+        pieces = jnp.concatenate([jnp.where(low, pieces, other), jnp.where(low, other, pieces)])
+        stride *= 2
+    return pieces
+
+
+def doubled_up(value, axis, dim):
+    return joined_along(doubled(value, axis), dim)
 
 
 def local(
@@ -78,7 +99,7 @@
     state_new_norm = hold_rate * moment_norm + mean_norm
     new_norm = weight_norm - learn_rate * state_new_norm
     copy_query, copy_key, copy_value, copy_mixed, copy_norm = (
-        lax.all_gather(new_query.astype(jnp.bfloat16), "replica", axis=0, tiled=True),
+        doubled_up(new_query.astype(jnp.bfloat16), "replica", 0),
         lax.all_gather(new_key.astype(jnp.bfloat16), "replica", axis=0, tiled=True),
         lax.all_gather(new_value.astype(jnp.bfloat16), "replica", axis=0, tiled=True),
         lax.all_gather(new_mixed.astype(jnp.bfloat16), "replica", axis=1, tiled=True),

time: 210 us -> 204 us (0.971)
  blocking collectives: 92.1 us -> 84.1 us
    all_gather x1 -> x0, blocking collectives: 14.8 us -> none  [local(): lax.all_gather(new_query.astype(jnp.bfloat16), 'replica', axis=0, tiled=T...]
    all_gather x1, blocking collectives: 15.3 us -> 22 us  [local(): lax.all_gather(new_value.astype(jnp.bfloat16), 'replica', axis=0, tiled=T...]
    unnamed x36 -> x35, local copies, waits for them, and re-layouts: 4.75 us -> 4.34 us
  transfers between devices with their start and end apart: 4 -> 6, of which waited for: 4 -> 4; matrix products, arithmetic and copies ran while one was open for 2% -> 4% of each run, Pallas kernels for 0% -> 0%
where the time goes in v1:
time: 204 us
  waiting for transfers between devices  90.2 us (44%)
  blocking collectives  84.1 us (41%)
  between operations  14 us (7%)
  other arithmetic  9.83 us (5%)
  local copies, waits for them, and re-layouts  4.34 us (2%)
    reduce_scatter x1, waiting for transfers between devices, local(): lax.psum_scatter(grad_query[0], 'replica', scatter_dimension=0, tiled=True)  27.1 us
    reduce_scatter x1, waiting for transfers between devices, local(): lax.psum_scatter(grad_mixed[0], 'replica', scatter_dimension=1, tiled=True)  27.1 us
    reduce_scatter x1, waiting for transfers between devices, local(): lax.psum_scatter(grad_key[0], 'replica', scatter_dimension=0, tiled=True)  26.8 us
    all_gather x1, blocking collectives, local(): lax.all_gather(new_value.astype(jnp.bfloat16), 'replica', axis=0, tiled=T...  22 us
    all_gather x1, blocking collectives, local(): lax.all_gather(new_key.astype(jnp.bfloat16), 'replica', axis=0, tiled=True)  16.2 us
    all_gather x1, blocking collectives, local(): lax.all_gather(new_mixed.astype(jnp.bfloat16), 'replica', axis=1, tiled=T...  14.7 us
    psum x1, blocking collectives, local(): whole_norm = lax.psum(grad_norm[0], 'replica')  13.5 us
    psum x1, blocking collectives, local(): lax.psum((jnp.sum(weight_query * weight_query, axis=1, keepdims=True), jn...  9.98 us
  transfers between devices with their start and end apart: 6, of which 4 were waited for; matrix products, arithmetic and copies ran while one was open for 4% of the time, Pallas kernels for 0%

profile of v1, /device:TPU:0, one launch (start us, length us, event | category | flops | bytes accessed | tf_op | source)
XLA Modules:
  0.0 203.5 jit_solution(11000045748837630089)
XLA Ops:
  7.2 0.0 reduce-scatter.9.cloned.1.call-start
  7.2 0.7 reduce-scatter.9.cloned.1.call-update
  7.9 0.0 reduce-scatter.11.cloned.1.call-start
  8.0 0.7 reduce-scatter.11.cloned.1.call-update
  8.7 0.0 reduce-scatter.5.cloned.1.call-start
  8.7 0.7 reduce-scatter.5.cloned.1.call-update
  9.4 0.0 reduce-scatter.7.cloned.1.call-start
  9.4 0.0 copy-start.12
  9.5 0.0 copy-start.13
  9.5 0.0 copy-start.14
  9.5 0.0 copy-start
  9.5 0.5 reduce-scatter.7.cloned.1.call-update
  10.0 0.0 copy-start.2
  10.0 0.1 copy-done.12
  10.1 13.5 %psum.71 = f32[1024]{0:T(1024)S(1)} all-reduce(f32[1024]{0:T(1024)S(1)} %bitcast.40), channel_id=1, replica_groups=mesh['job'=2,'replica'=4,'model'=4] {'replica'}, use_global_device_ids=true, to_apply=%region_20.0 | all-reduce | flops 1024 | bytes 8192 | tf_op jit(solution)/shard_map/psum | solution.py:54
  23.6 0.0 copy-done.13
  23.6 0.0 copy-done.14
  23.6 0.6 fusion
  24.3 7.7 %all-gather = bf16[4,1,256]{2,1,0:T(2,128)(2,1)S(1)} all-gather(bf16[1,1,256]{2,1,0:T(2,128)(2,1)S(1)} %reshape.42), channel_id=1, replica_groups=mesh['job'=2,'replica'=4,'model'=4] {'replica'}, dimensions={0}, use_global_device_ids=true | all-gather | bytes 2560 | tf_op jit(solution)/shard_map/all_gather | solution.py:106
  32.0 0.6 copy.30
  32.6 0.0 copy-done
  32.6 0.0 copy-start.3
  32.6 0.1 multiply_reduce_fusion.7
  32.7 0.0 copy-done.2
  32.7 0.0 copy-start.1
  32.7 0.1 multiply_reduce_fusion.3
  32.9 0.7 copy-done.3
  33.6 0.1 copy-done.1
  33.7 0.1 multiply_reduce_fusion.5
  33.8 6.6 %reduce-scatter.9.cloned.1.call-done = f32[256,256]{1,0:T(8,128)} async-done(((f32[1024,256]{1,0:T(8,128)}), f32[256,256]{1,0:T(8,128)}) %reduce-scatter.9.cloned.1.call-update) | async-done | bytes 262160 | tf_op jit(solution)/shard_map/reduce_scatter | solution.py:51
  40.4 1.1 multiply_reduce_fusion.2
  41.5 27.1 %reduce-scatter.11.cloned.1.call-done = f32[256,256]{1,0:T(8,128)} async-done(((f32[256,1024]{1,0:T(8,128)}), f32[256,256]{1,0:T(8,128)}) %reduce-scatter.11.cloned.1.call-update) | async-done | bytes 262160 | tf_op jit(solution)/shard_map/reduce_scatter | solution.py:52
  68.6 1.0 multiply_reduce_fusion
  69.6 27.1 %reduce-scatter.5.cloned.1.call-done = f32[256,256]{1,0:T(8,128)} async-done(((f32[1024,256]{1,0:T(8,128)}), f32[256,256]{1,0:T(8,128)}) %reduce-scatter.5.cloned.1.call-update) | async-done | bytes 262160 | tf_op jit(solution)/shard_map/reduce_scatter | solution.py:49
  96.7 0.0 copy-start.7
  96.7 1.1 multiply_reduce_fusion.6
  97.8 26.8 %reduce-scatter.7.cloned.1.call-done = f32[256,256]{1,0:T(8,128)} async-done(((f32[1024,256]{1,0:T(8,128)}), f32[256,256]{1,0:T(8,128)}) %reduce-scatter.7.cloned.1.call-update) | async-done | bytes 262160 | tf_op jit(solution)/shard_map/reduce_scatter | solution.py:50
  124.7 1.1 multiply_reduce_fusion.4
  125.7 10.0 %all-reduce = (f32[256,1]{0,1:T(1,128)S(1)}, f32[256,1]{0,1:T(1,128)S(1)}, f32[256,1]{0,1:T(1,128)S(1)}, f32[256,1]{0,1:T(1,128)S(1)}, f32[256,1]{0,1:T(1,128)S(...) all-reduce(f32[256,1]{0,1:T(1,128)S(1)} %bitcast.38, ...), channel_id=1, replica_groups=mesh['job'=2,'replica'=4,'model'=4] {'model'}, use_global_device_ids=true, to_apply=%region_4.0 | all-reduce | flops 2048 | bytes 16384 | tf_op jit(solution)/shard_map/psum | solution.py:74
  135.7 0.0 copy-done.8
  135.7 0.0 copy-done.7
  135.7 0.0 copy-start.6
  135.8 0.0 copy-start.9
  135.8 0.9 convert_bitcast_fusion
  136.7 0.0 collective-permute-start
  136.7 0.0 copy-done.6
  136.7 0.1 copy-done.9
  136.8 0.9 fusion.3
  137.7 0.0 copy-done.4
  137.7 0.1 copy-done.10
  137.9 0.9 fusion.2
  138.8 0.0 copy-done.5
  138.8 0.1 copy-done.11
  138.9 0.8 fusion.1
  139.8 16.2 %all_gather.12 = bf16[1024,256]{1,0:T(8,128)(2,1)S(1)} all-gather(bf16[256,256]{1,0:T(8,128)(2,1)S(1)} %get-tuple-element.32), channel_id=1, replica_groups=mesh['job'=2,'replica'=4,'model'=4] {'replica'}, dimensions={0}, use_global_device_ids=true | all-gather | bytes 655360 | tf_op jit(solution)/shard_map/all_gather | solution.py:103
  156.0 0.0 collective-permute-done
  156.0 1.0 collective-permute-start.1
  157.0 22.0 %all_gather.13 = bf16[1024,256]{1,0:T(8,128)(2,1)S(1)} all-gather(bf16[256,256]{1,0:T(8,128)(2,1)S(1)} %get-tuple-element.29), channel_id=1, replica_groups=mesh['job'=2,'replica'=4,'model'=4] {'replica'}, dimensions={0}, use_global_device_ids=true | all-gather | bytes 655360 | tf_op jit(solution)/shard_map/all_gather | solution.py:104
  179.0 14.7 %all_gather.14 = bf16[256,1024]{1,0:T(8,128)(2,1)S(1)} all-gather(bf16[256,256]{1,0:T(8,128)(2,1)S(1)} %get-tuple-element.26), channel_id=1, replica_groups=mesh['job'=2,'replica'=4,'model'=4] {'replica'}, dimensions={1}, use_global_device_ids=true | all-gather | bytes 655360 | tf_op jit(solution)/shard_map/all_gather | solution.py:105
  193.7 0.0 collective-permute-done.1
  193.8 0.8 pad_maximum_fusion
  194.6 0.8 copy.34
  195.4 0.8 copy.35
  196.2 0.8 copy.36
  (14 shorter events, 0.2 us)
Async XLA Ops:
  7.2 33.2 %reduce-scatter.9.cloned.1.call-start = ((), (), s32[]{:S(2)}) async-start(), calls=%async_computation.6 | async-start | bytes 1310720 | tf_op jit(solution)/shard_map/reduce_scatter | solution.py:51
  7.9 60.6 %reduce-scatter.11.cloned.1.call-start = ((), (), s32[]{:S(2)}) async-start(), calls=%async_computation.7 | async-start | bytes 1310720 | tf_op jit(solution)/shard_map/reduce_scatter | solution.py:52
  8.7 88.0 %reduce-scatter.5.cloned.1.call-start = ((), (), s32[]{:S(2)}) async-start(), calls=%async_computation.4 | async-start | bytes 1310720 | tf_op jit(solution)/shard_map/reduce_scatter | solution.py:49
  9.4 115.2 %reduce-scatter.7.cloned.1.call-start = ((), (), s32[]{:S(2)}) async-start(), calls=%async_computation.5 | async-start | bytes 1310720 | tf_op jit(solution)/shard_map/reduce_scatter | solution.py:50
  9.4 0.7 copy-start.12
  9.5 14.1 %copy-start.13 = (f32[256]{0:T(256)S(1)}, f32[256]{0:T(256)}, u32[]{:S(2)}) copy-start(f32[256]{0:T(256)} %param.24) | copy-start | bytes 3076
  9.5 14.1 %copy-start.14 = (f32[256]{0:T(256)S(1)}, f32[256]{0:T(256)}, u32[]{:S(2)}) copy-start(f32[256]{0:T(256)} %param.29) | copy-start | bytes 3076
  9.5 23.1 %copy-start = (f32[256,256]{1,0:T(8,128)S(1)}, f32[256,256]{1,0:T(8,128)}, u32[]{:S(2)}) copy-start(f32[256,256]{1,0:T(8,128)} %param.20) | copy-start | bytes 786436
  10.0 22.7 %copy-start.2 = (f32[256,256]{1,0:T(8,128)S(1)}, f32[256,256]{1,0:T(8,128)}, u32[]{:S(2)}) copy-start(f32[256,256]{1,0:T(8,128)} %param.22) | copy-start | bytes 786436
  32.6 1.0 copy-start.3
  32.7 1.0 copy-start.1
  69.6 66.2 %copy-start.8 = (f32[256,256]{1,0:T(8,128)S(1)}, f32[256,256]{1,0:T(8,128)}, u32[]{:S(2)}) copy-start(f32[256,256]{1,0:T(8,128)} %param.25) | copy-start | bytes 786436
  96.7 39.1 %copy-start.7 = (f32[256,256]{1,0:T(8,128)S(1)}, f32[256,256]{1,0:T(8,128)}, u32[]{:S(2)}) copy-start(f32[256,256]{1,0:T(8,128)} %reduce-scatter.5.cloned.1.call-done) | copy-start | bytes 786436
  135.7 1.0 copy-start.6
  135.8 1.0 copy-start.9
  136.7 19.3 %collective-permute-start = (bf16[1,256,256]{2,1,0:T(8,128)(2,1)S(1)}, bf16[1,256,256]{2,1,0:T(8,128)(2,1)S(1)}, u32[]{:S(2)}, u32[]{:S(2)}) collective-permute-start(bf16[1,256,256]{2,1,0:T(8,128)(2,1)S(1)} %get-tuple-element.35), channel_id=1, source_target_pairs={{0,4},{4,0},{8,12},{12,8},{1,5},{5,1},{9,13},{13,9},{2,6},{6,2},{1... | collective-permute-start | bytes 393224 | tf_op jit(solution)/shard_map/ppermute | solution.py:20
  136.8 0.9 copy-start.4
  136.8 1.1 copy-start.10
  137.9 0.9 copy-start.5
  137.9 1.1 copy-start.11
  156.0 37.7 %collective-permute-start.1 = (bf16[2,256,256]{2,1,0:T(8,128)(2,1)S(1)}, bf16[2,256,256]{2,1,0:T(8,128)(2,1)S(1)}, u32[]{:S(2)}, u32[]{:S(2)}) collective-permute-start(bf16[2,256,256]{2,1,0:T(8,128)(2,1)S(1)} %pad_maximum_fusion.1), channel_id=1, source_target_pairs={{0,8},{4,12},{8,0},{12,4},{1,9},{5,13},{9,1},{13,5},{2,10},{6,14},... | collective-permute-start | bytes 786440 | tf_op jit(solution)/shard_map/ppermute | solution.py:20
Sparse Core Ops, SparseCore 0:
  10.3 30.1 reduce-scatter.8
  42.7 25.7 reduce-scatter.10
  70.9 25.7 reduce-scatter.4
  98.8 25.7 reduce-scatter.6
